TPU v7x, 512 devices: a whole 4x4x16 slice. The times are simulated.
512 devices in a mesh: group: 16 (over y, x), member: 32 (over z, core).
Axes of the slice: x: 4, y: 4, z: 16, core: 2. Of those that a mesh axis runs over, the one named last changes fastest.
Arguments:
- tokens: bfloat16 [65536, 2048], P(('group', 'member')), may hold values from -6 to 6
- cotangent: bfloat16 [65536, 2048], P(('group', 'member')), may hold values from -6 to 6
- w_gate: bfloat16 [2048, 512], P('member'), may hold values from -0.125 to 0.125
- w_up: bfloat16 [2048, 512], P('member'), may hold values from -0.125 to 0.125
- w_down: bfloat16 [2048, 512], P('member'), may hold values from -0.125 to 0.125
- basis: float32 [2048, 256], P('member'), may hold values from -0.088388348 to 0.088388348
- first_moment: float32 [3, 256, 512], P(None, 'member'), may hold values from -3 to 3
- second_moment: float32 [3, 256, 512], P(None, 'member'), may hold values from 0.1 to 2
Outputs:
- input_grad: bfloat16 [65536, 2048], P(('group', 'member'))
- new_first: float32 [3, 256, 512], P(None, 'member')
- new_second: float32 [3, 256, 512], P(None, 'member')
- updates: float32 [3, 2048, 512], P(None, 'member')
All inputs are finite; a program needn't handle non-finite values.
Results may differ from a plain program's by a relative error of at most 0.008.
Values may be sent and summed in bfloat16 or wider, within the bound.
A program may use at most 64 MiB of HBM per device.

v0:
```python
import math

import jax
import jax.numpy as jnp
from jax import lax
from jax.sharding import Mesh
from jax.sharding import PartitionSpec as P

FF = 512
RANK = 256
MEMBER = ("member_0", "member_1")
GROUP_MEMBER = ("group", "member_0", "member_1")


def in_one_piece(arrays, axis, dim, along):
    both = jnp.concatenate(arrays, axis=along)
    whole, at, gathered = (lax.all_gather(both, axis, axis=dim, tiled=True), 0, [])
    for a in arrays:
        gathered.append(lax.slice_in_dim(whole, at, at + a.shape[along], axis=along))
        at += a.shape[along]
    return tuple(gathered)


def joined_along(pieces, dim):
    pieces = jnp.moveaxis(pieces, 0, dim)
    shape = pieces.shape
    return pieces.reshape(*shape[:dim], shape[dim] * shape[dim + 1], *shape[dim + 2 :])


def copy_for_each(value, axis):
    peers = lax.axis_size(axis)
    return lax.all_to_all(
        jnp.broadcast_to(value[None], (peers, *value.shape)), axis, 0, 0, tiled=True
    )


def gathered_copies(value, axis, dim):
    return joined_along(copy_for_each(value, axis), dim)


def in_blocks(value, dim, peers):
    before, after = (value.shape[:dim], value.shape[dim + 1 :])
    return jnp.moveaxis(value.reshape(*before, peers, -1, *after), dim, 0)


def sum_at_owner(value, axis, dim):
    pieces = in_blocks(value, dim, lax.axis_size(axis))
    arrived = lax.all_to_all(pieces, axis, split_axis=0, concat_axis=0, tiled=True)
    return arrived.sum(axis=0)


def of_everyone(value, axis):
    return copy_for_each(value, axis).sum(axis=0)


def gather_in_order(value, axes, order):
    pieces = value[None]
    for k in order:
        pieces = lax.all_gather(pieces, axes[k], axis=0, tiled=True)
    block = [lax.axis_size(axes[k]) for k in reversed(order)]
    pieces = pieces.reshape(*block, *value.shape)
    turned = sorted(range(len(order)), key=lambda place: order[len(order) - 1 - place])
    return pieces.transpose(*turned, *range(len(order), pieces.ndim)).reshape(-1, *value.shape)


def whole_of(value, axes, order, dim):
    return joined_along(gather_in_order(value, axes, order), dim)


def contract_rows(left, right):
    return lax.dot_general(
        left, right, (((0,), (0,)), ((), ())), preferred_element_type=jnp.float32
    )


def contract_cols(left, right):
    return lax.dot_general(
        left, right, (((1,), (1,)), ((), ())), preferred_element_type=jnp.float32
    )


def split_parts(values):
    high_part = values.astype(jnp.bfloat16)
    low_part = (values - high_part.astype(jnp.float32)).astype(jnp.bfloat16)
    return (high_part, low_part)


def local(tokens, cotangent, w_gate, w_up, w_down, basis, first_moment, second_moment):
    full_gate, full_up, full_down = in_one_piece((w_gate, w_up, w_down), MEMBER, 0, 1)
    gate = jnp.dot(tokens, full_gate, preferred_element_type=jnp.float32)
    up = jnp.dot(tokens, full_up, preferred_element_type=jnp.float32)
    dhid = jnp.dot(cotangent, full_down, preferred_element_type=jnp.float32)
    sig = jax.nn.sigmoid(gate)
    silu = gate * sig
    hidden = (silu * up).astype(jnp.bfloat16)
    dgate = (dhid * up * sig * (1.0 + gate * (1.0 - sig))).astype(jnp.bfloat16)
    dup = (dhid * silu).astype(jnp.bfloat16)
    dx_full = contract_cols(dgate, full_gate) + contract_cols(dup, full_up)
    input_grad = dx_full.astype(jnp.bfloat16)
    full_basis = gathered_copies(basis, MEMBER, 0)
    highest = lax.Precision.HIGHEST
    basis_high, basis_low = split_parts(full_basis)
    x_proj = jnp.dot(tokens, basis_high, preferred_element_type=jnp.float32) + jnp.dot(
        tokens, basis_low, preferred_element_type=jnp.float32
    )
    y_proj = jnp.dot(cotangent, basis_high, preferred_element_type=jnp.float32) + jnp.dot(
        cotangent, basis_low, preferred_element_type=jnp.float32
    )
    x_high, x_low = split_parts(x_proj)
    y_high, y_low = split_parts(y_proj)
    low_gate = contract_rows(x_high, dgate) + contract_rows(x_low, dgate)
    low_up = contract_rows(x_high, dup) + contract_rows(x_low, dup)
    low_down = contract_rows(y_high, hidden) + contract_rows(y_low, hidden)
    local_low = jnp.stack([low_gate, low_up, low_down])
    partial_rows = sum_at_owner(local_low, MEMBER, 1)
    share = of_everyone(partial_rows, "group")
    squares = of_everyone(jnp.sum(share * share), MEMBER)
    limit = math.sqrt(3.0 * RANK * FF)
    factor = jnp.minimum(1.0, limit / jnp.sqrt(squares + 1e-06))
    grad_low = factor * share
    new_first = 0.5 * first_moment + 0.5 * grad_low
    new_second = 0.9 * second_moment + 0.1 * grad_low * grad_low
    step = (new_first / (jnp.sqrt(new_second) + 1e-08)).astype(jnp.bfloat16)
    updates = jnp.einsum(
        "dr,krf->kdf",
        basis,
        whole_of(step, MEMBER, (0, 1), 1).astype(jnp.float32),
        precision=highest,
    )
    return (input_grad, new_first, new_second, updates)


def solution(mesh):
    torus = Mesh(
        mesh.devices.reshape(mesh.shape["group"], 16, 2), ("group", "member_0", "member_1")
    )
    placed = (
        P(GROUP_MEMBER, None),
        P(GROUP_MEMBER, None),
        P(MEMBER, None),
        P(MEMBER, None),
        P(MEMBER, None),
        P(MEMBER, None),
        P(None, MEMBER, None),
        P(None, MEMBER, None),
    )
    return jax.shard_map(
        local,
        mesh=torus,
        in_specs=placed,
        out_specs=(
            P(GROUP_MEMBER, None),
            P(None, MEMBER, None),
            P(None, MEMBER, None),
            P(None, MEMBER, None),
        ),
        check_vma=False,
    )
```

profile of v0, /device:TPU:1, one launch (start us, length us, event | category | flops | bytes accessed | tf_op | source)
XLA Modules:
  0.0 337.4 jit_solution(16014299406178635966)
XLA Ops:
  7.2 1.6 pad_maximum_fusion
  8.9 1.1 broadcast_in_dim.8
  10.0 137.4 %all_to_all.21 = f32[32,64,256]{2,1,0:T(8,128)S(1)} all-to-all(f32[32,64,256]{2,1,0:T(8,128)S(1)} %broadcast_in_dim.8), channel_id=1, replica_groups=mesh['group'=16,'member_0'=16,'member_1'=2] {'member_0','member_1'}, dimensions={0} | all-to-all | bytes 4194304 | tf_op jit(solution)/shard_map/all_to_all | solution.py:32
  147.4 0.3 fusion.3
  147.7 0.8 copy-done.2
  148.4 0.3 fusion.37
  148.8 0.3 fusion.36
  149.1 0.3 fusion.24
  149.4 0.3 fusion.23
  149.8 12.7 %all-gather.3.cloned.1.call-done = bf16[2048,1536]{1,0:T(8,128)(2,1)} async-done(((bf16[64,1536]{1,0:T(8,128)(2,1)}), bf16[2048,1536]{1,0:T(8,128)(2,1)}) %all-gather.3.cloned.1.call-update) | async-done | bytes 6291472 | tf_op jit(solution)/shard_map/all_gather | solution.py:17
  162.4 2.5 fusion.17
  164.9 2.3 fusion.20
  167.3 0.8 multiply_convert_fusion
  168.0 0.2 fusion.29
  168.3 0.3 fusion.11
  168.8 0.3 fusion.12
  169.3 0.3 fusion.13
  169.7 85.5 %all_to_all.22 = f32[32,3,8,512]{3,2,1,0:T(8,128)S(1)} all-to-all(f32[32,3,8,512]{3,2,1,0:T(8,128)S(1)} %maximum_bitcast_fusion), channel_id=1, replica_groups=mesh['group'=16,'member_0'=16,'member_1'=2] {'member_0','member_1'}, dimensions={0} | all-to-all | bytes 3145728 | tf_op jit(solution)/shard_map/all_to_all | solution.py:48
  255.3 1.0 broadcast_in_dim.9
  256.3 6.8 %all-to-all-start.2 = ((f32[16,3,8,512]{3,2,1,0:T(8,128)}), f32[16,3,8,512]{3,2,1,0:T(8,128)S(1)}, u32[]{:S(2)}, u32[]{:S(2)}) async-start(f32[16,3,8,512]{3,2,1,0:T(8,128)} %broadcast_in_dim.9), calls=%async_computation.2 | async-start | bytes 1572864 | tf_op jit(solution)/shard_map/all_to_all | solution.py:32
  263.1 2.4 fusion.4
  265.5 11.0 %all-to-all-done.2 = f32[16,3,8,512]{3,2,1,0:T(8,128)S(1)} async-done(((f32[16,3,8,512]{3,2,1,0:T(8,128)}), f32[16,3,8,512]{3,2,1,0:T(8,128)S(1)}, u32[]{:S(2)}, u32[]{:S(2)}) %all-to-all-start.2) | async-done | bytes 786464 | tf_op jit(solution)/shard_map/all_to_all | solution.py:32
  276.5 0.6 multiply_reduce_fusion
  277.1 1.3 broadcast_in_dim.10
  278.4 5.5 %all-to-all-start.3 = ((f32[32,1,1]{2,1,0:T(1,128)}), f32[32,1,1]{2,1,0:T(1,128)S(1)}, u32[]{:S(2)}, u32[]{:S(2)}) async-start(f32[32,1,1]{2,1,0:T(1,128)} %broadcast_in_dim.10), calls=%async_computation.3 | async-start | bytes 32768 | tf_op jit(solution)/shard_map/all_to_all | solution.py:32
  283.9 3.2 fusion
  287.1 8.6 %all-to-all-done.3 = f32[32,1,1]{2,1,0:T(1,128)S(1)} async-done(((f32[32,1,1]{2,1,0:T(1,128)}), f32[32,1,1]{2,1,0:T(1,128)S(1)}, u32[]{:S(2)}, u32[]{:S(2)}) %all-to-all-start.3) | async-done | bytes 160 | tf_op jit(solution)/shard_map/all_to_all | solution.py:32
  295.8 0.6 reduce_sum.39
  297.1 0.7 divide_convert_fusion
  297.8 21.5 %all-gather = bf16[48,8,512]{2,1,0:T(8,128)(2,1)S(1)} all-gather(bf16[3,8,512]{2,1,0:T(8,128)(2,1)S(1)} %get-tuple-element.4), channel_id=2, replica_groups=mesh['group'=16,'member_0'=16,'member_1'=2] {'member_0'}, dimensions={0}, use_global_device_ids=true | all-gather | bytes 417792 | tf_op jit(solution)/shard_map/all_gather | solution.py:59
  319.2 10.0 %all_gather.11 = bf16[32,3,8,512]{3,2,1,0:T(8,128)(2,1)S(1)} all-gather(bf16[16,3,8,512]{3,2,1,0:T(8,128)(2,1)S(1)} %bitcast.70), channel_id=1, replica_groups=mesh['group'=16,'member_0'=16,'member_1'=2] {'member_1'}, dimensions={0}, use_global_device_ids=true | all-gather | bytes 1179648 | tf_op jit(solution)/shard_map/all_gather | solution.py:59
  329.3 1.3 convolution_bitcast_fusion
  (19 shorter events, 1.0 us)
Async XLA Ops:
  7.2 141.6 %copy-start = (bf16[128,2048]{1,0:T(8,128)(2,1)S(1)}, bf16[128,2048]{1,0:T(8,128)(2,1)}, u32[]{:S(2)}) copy-start(bf16[128,2048]{1,0:T(8,128)(2,1)} %param.8) | copy-start | bytes 1572868
  7.2 155.2 %all-gather.3.cloned.1.call-start = ((), (), s32[]{:S(2)}) async-start(), calls=%async_computation.4 | async-start | bytes 6488064 | tf_op jit(solution)/shard_map/all_gather | solution.py:17
  147.4 1.0 copy-start.2
  162.4 4.8 %copy-start.1 = (bf16[2048,1536]{1,0:T(8,128)(2,1)S(1)}, bf16[2048,1536]{1,0:T(8,128)(2,1)}, u32[]{:S(2)}) copy-start(bf16[2048,1536]{1,0:T(8,128)(2,1)} %all-gather.3.cloned.1.call-done) | copy-start | bytes 18874372
  256.3 20.2 %all-to-all-start.2 = ((f32[16,3,8,512]{3,2,1,0:T(8,128)}), f32[16,3,8,512]{3,2,1,0:T(8,128)S(1)}, u32[]{:S(2)}, u32[]{:S(2)}) async-start(f32[16,3,8,512]{3,2,1,0:T(8,128)} %broadcast_in_dim.9), calls=%async_computation.2 | async-start | bytes 1572864 | tf_op jit(solution)/shard_map/all_to_all | solution.py:32
  276.5 20.6 %copy-start.4 = (f32[3,8,512]{2,1,0:T(8,128)S(1)}, f32[3,8,512]{2,1,0:T(8,128)}, u32[]{:S(2)}) copy-start(f32[3,8,512]{2,1,0:T(8,128)} %param.15) | copy-start | bytes 147460
  276.5 20.6 %copy-start.5 = (f32[3,8,512]{2,1,0:T(8,128)S(1)}, f32[3,8,512]{2,1,0:T(8,128)}, u32[]{:S(2)}) copy-start(f32[3,8,512]{2,1,0:T(8,128)} %param.14) | copy-start | bytes 147460
  278.4 17.3 %all-to-all-start.3 = ((f32[32,1,1]{2,1,0:T(1,128)}), f32[32,1,1]{2,1,0:T(1,128)S(1)}, u32[]{:S(2)}, u32[]{:S(2)}) async-start(f32[32,1,1]{2,1,0:T(1,128)} %broadcast_in_dim.10), calls=%async_computation.3 | async-start | bytes 32768 | tf_op jit(solution)/shard_map/all_to_all | solution.py:32
  287.1 42.2 %copy-start.3 = (f32[64,256]{1,0:T(8,128)S(1)}, f32[64,256]{1,0:T(8,128)}, u32[]{:S(2)}) copy-start(f32[64,256]{1,0:T(8,128)} %param.13) | copy-start | bytes 196612
Sparse Core Ops, SparseCore 0:
  10.7 151.6 all-gather.2
where the time goes:
time: 338 us; the launch traced here: 337 us
  blocking collectives  254 us (75%)
  waiting for transfers between devices  32.3 us (10%)
  matrix products  15.2 us (4%)
  between operations  14.9 us (4%)
  starting transfers between devices  12.3 us (4%)
  local copies, waits for them, and re-layouts  4.19 us (1%)
  other arithmetic  4.12 us (1%)
    all_to_all x1, blocking collectives, copy_for_each(): lax.all_to_all(jnp.broadcast_to(value[None], (peers, *value.shape)), axis...  137 us
    all_to_all x1, blocking collectives, sum_at_owner(): lax.all_to_all(pieces, axis, split_axis=0, concat_axis=0, tiled=True)  85.5 us
    all_gather x2, blocking collectives, gather_in_order(): pieces = lax.all_gather(pieces, axes[k], axis=0, tiled=True)  31.4 us
    all_to_all x2, waiting for transfers between devices, copy_for_each(): lax.all_to_all(jnp.broadcast_to(value[None], (peers, *value.shape)), axis...  19.6 us
    all_gather x1, waiting for transfers between devices, in_one_piece(): lax.all_gather(both, axis, axis=dim, tiled=True)  12.7 us
    all_to_all x2, starting transfers between devices, copy_for_each(): lax.all_to_all(jnp.broadcast_to(value[None], (peers, *value.shape)), axis...  12.3 us
  transfers between devices with their start and end apart: 3, of which 3 were waited for; matrix products, arithmetic and copies ran while one was open for 2% of the time, Pallas kernels for 0%

commit v1 on v0

v1 whole, which is shorter than its diff:
```python
import functools
import math

import jax
import jax.numpy as jnp
from jax import lax
from jax.experimental import pallas as pl
from jax.experimental.pallas import tpu as pltpu
from jax.sharding import PartitionSpec as P

BF = jnp.bfloat16
F32 = jnp.float32
MESH = pl.DeviceIdType.MESH

D = 2048
FF = 512
RANK = 256
TOK = 128
NX, NY, NZ = 4, 4, 16
NP = NX * NY
HF = FF // 2
HR = RANK // 2
ROWS = 64
PW = 3 * HF + HR
EPS_LIMIT = math.sqrt(3.0 * RANK * FF)

G0, U0, B0, D0 = 0, HF, 2 * HF, 2 * HF + HR


class Sems:
    def __init__(self, ref, count):
        self.ref, self.count, self.used = ref, count, 0

    def take(self):
        self.used += 1
        assert self.used <= self.count
        return self.ref.at[self.used - 1]


NSEND = 240


def kernel(
    tok_hbm, cot_hbm, wg_hbm, wu_hbm, wd_hbm, bas_hbm, fm_hbm, sm_hbm,
    dx_hbm, nf_hbm, ns_hbm, up_hbm,
    toks, cots, wbuf, wgv, wuv, wdv, basv, fmv, smv,
    pk, bp, msend, mrecv, mbuf,
    accx, accy, xpb, dgu, hid, lsend, lrecv,
    dxp, dxr, dxo, t0b, nearb, t1b, farb,
    sqo, sqp, sqb, lrow, lall, loth, sbuf, uov, ucv, nfv, nsv,
    lsem, ssem, zsem, xysem, psem, msem, rsem, nsem, fsem, qsem, rowsem, stsem,
):
    g = lax.axis_index("group")
    m = lax.axis_index("member")
    y, x = lax.div(g, NX), lax.rem(g, NX)
    z, c = lax.div(m, 2), lax.rem(m, 2)
    o = 1 - c
    p = g

    def dev(dx=0, dy=0, dz=0):
        yy = lax.rem(y + dy + NY, NY)
        xx = lax.rem(x + dx + NX, NX)
        zz = lax.rem(z + dz + NZ, NZ)
        return (yy * NX + xx, zz * 2 + c)

    partner = (g, z * 2 + o)

    local = []

    def load(src, dst):
        cp = pltpu.make_async_copy(src, dst, lsem.at[len(local)])
        cp.start()
        local.append(cp)
        return cp

    ld_w = [load(wg_hbm, wgv), load(wu_hbm, wuv), load(wd_hbm, wdv), load(bas_hbm, basv)]
    ld_t = [load(tok_hbm, toks.at[c]), load(cot_hbm, cots.at[c])]
    ld_m = [load(fm_hbm, fmv), load(sm_hbm, smv)]

    barrier = pltpu.get_barrier_semaphore()
    near = [partner]
    near += [dev(dz=1), dev(dz=-1), dev(dz=2), dev(dz=-2)]
    near += [dev(dx=1), dev(dx=-1), dev(dx=2)]
    near += [dev(dy=1), dev(dy=-1), dev(dy=2)]
    for d in near:
        pl.semaphore_signal(barrier, inc=1, device_id=d, device_id_type=MESH)

    sends = []
    takes = Sems(ssem, NSEND)

    def remote(src, dst, rsem_, d):
        cp = pltpu.make_async_remote_copy(
            src_ref=src, dst_ref=dst, send_sem=takes.take(), recv_sem=rsem_,
            device_id=d, device_id_type=MESH,
        )
        cp.start()
        sends.append(cp)
        return cp

    def arrived(dst, rsem_):
        pltpu.make_async_remote_copy(
            src_ref=dst, dst_ref=dst, send_sem=ssem.at[0], recv_sem=rsem_,
            device_id=partner, device_id_type=MESH,
        ).wait_recv()

    for cp in ld_w:
        cp.wait()
    pr = lax.broadcasted_iota(jnp.int32, (RANK, RANK), 0)
    pc = lax.broadcasted_iota(jnp.int32, (RANK, RANK), 1)
    perm = (pr == (pc & (NZ - 1)) * NP + (pc >> 4)).astype(F32).astype(BF)
    bas = basv[...]
    bh = bas.astype(BF)
    bl = (bas - bh.astype(F32)).astype(BF)
    bp[c, 0] = jnp.dot(bh, perm, preferred_element_type=F32).astype(BF)
    bp[c, 1] = jnp.dot(bl, perm, preferred_element_type=F32).astype(BF)

    def al(v, n):
        return pl.multiple_of(v, n)

    own_rows = pl.ds(al(c * ROWS, ROWS), ROWS)
    for half, put in ((o, "partner"), (c, "own")):
        fs = pl.ds(al(half * HF, HF), HF)
        rs = pl.ds(al(half * HR, HR), HR)
        for col, width, val in (
            (G0, HF, wgv[:, fs]), (U0, HF, wuv[:, fs]), (B0, HR, bp[c, 0, :, rs]), (D0, HF, wdv[:, fs]),
        ):
            if put == "partner":
                pk[:, col : col + width] = val
            else:
                wbuf[z, own_rows, col : col + width] = val

    pl.semaphore_wait(barrier, len(near))

    remote(pk, wbuf.at[z, own_rows], psem.at[0], partner)

    def roff(h, dx=0, dy=0):
        if h == 0:
            return al(16 * lax.rem(x + dx + NX, NX), 16)
        return al(64 + 16 * lax.rem(y + dy + NY, NY), 16)

    def zchunk(zo, row):
        return wbuf.at[zo, pl.ds(row, 16)]

    def zsend(zo, h, row, dz, rel):
        remote(zchunk(zo, row), zchunk(zo, row), zsem.at[h, rel], dev(dz=dz))

    own_off = al((1 - c) * (16 * x) + c * (64 + 16 * y), 16)
    oth_off = al(c * (16 * x) + (1 - c) * (64 + 16 * y), 16)
    for h, off in ((c, own_off), (o, oth_off)):
        if h is o:
            arrived(wbuf.at[z, pl.ds(al(o * ROWS, ROWS), ROWS)], psem.at[0])
        for dz in (1, -1, 2, -2):
            zsend(z, h, off, dz, dz % NZ)

    for cp in ld_t:
        cp.wait()
    remote(toks.at[c], toks.at[c], psem.at[1], partner)
    remote(cots.at[c], cots.at[c], psem.at[2], partner)
    remote(bp.at[c], bp.at[c], psem.at[3], partner)

    for cp in ld_m:
        cp.wait()
    prow = lax.rem(p, 8)
    pcore = lax.div(p, 8)
    zero = jnp.zeros((2, HF), F32)
    msend[6:8, :] = zero
    mbuf[z, 6:8, :] = zero
    for i, mv in enumerate((fmv, smv)):
        for k in range(3):
            msend[3 * i + k : 3 * i + k + 1, :] = mv[k, pl.ds(prow, 1), pl.ds(al(o * HF, HF), HF)]
            mbuf[z, 3 * i + k : 3 * i + k + 1, :] = mv[k, pl.ds(prow, 1), pl.ds(al(c * HF, HF), HF)]
    remote(msend, mrecv, psem.at[4], partner)

    def origin(rel):
        return lax.rem(z - rel + NZ, NZ)

    def z_arrive(s):
        for d in (0, 1):
            rel = s if d == 0 else NZ - s
            zo = origin(rel)
            sgn = 1 if d == 0 else -1
            hs = (0, 1) if s < 8 else ((0,) if d == 0 else (1,))
            for h in hs:
                arrived(zchunk(zo, roff(h)), zsem.at[h, rel])
                if s % 2 == 0 and s < 8:
                    zsend(zo, h, roff(h), sgn, (rel + sgn) % NZ)
                    if s + 2 < 8 or (d == 0) == (h == 0):
                        zsend(zo, h, roff(h), 2 * sgn, (rel + 2 * sgn) % NZ)
            for h in hs:
                for e in (1, -1):
                    t = dev(dx=e) if h == 0 else dev(dy=e)
                    remote(zchunk(zo, roff(h)), zchunk(zo, roff(h)), xysem.at[h, 0 if e == 1 else 1, rel], t)

    def pieces(s):
        if s == 8:
            return [(8, (0, 1))]
        return [(s, (0, 0)), (NZ - s, (1, 1))]

    def step_of(h, e):
        return roff(h, dx=e) if h == 0 else roff(h, dy=e)

    def xy_direct(s):
        for rel, ways in pieces(s):
            zo = origin(rel)
            for h in (0, 1):
                way = ways[h]
                e = -1 if way == 0 else 1
                ch = zchunk(zo, step_of(h, e))
                arrived(ch, xysem.at[h, way, rel])
                t = dev(dx=-e) if h == 0 else dev(dy=-e)
                remote(ch, ch, xysem.at[h, 2, rel], t)

    def xy_rest(s):
        for rel, ways in pieces(s):
            zo = origin(rel)
            for h in (0, 1):
                way = 1 - ways[h]
                e = -1 if way == 0 else 1
                arrived(zchunk(zo, step_of(h, e)), xysem.at[h, way, rel])
                arrived(zchunk(zo, step_of(h, 2)), xysem.at[h, 2, rel])

    def multiply(rel, first=False):
        zo = origin(rel)
        cols = pl.ds(al(zo * 128, 128), 128)
        tk = toks[:, :, cols].reshape(2 * TOK, 128)
        ck = cots[:, :, cols].reshape(2 * TOK, 128)
        ax = jnp.dot(tk, wbuf[zo, :, 0:D0], preferred_element_type=F32)
        ay = jnp.dot(ck, wbuf[zo, :, B0:PW], preferred_element_type=F32)
        if first:
            accx[...] = ax
            accy[...] = ay
        else:
            accx[...] += ax
            accy[...] += ay

    def finish(s):
        xy_rest(s)
        for rel, _ in pieces(s):
            multiply(rel)

    for s in range(1, 9):
        z_arrive(s)
        if s == 6:
            arrived(mrecv, psem.at[4])
            mine = pcore == c
            mbuf[z] = jnp.where(mine, mbuf[z], mrecv[...])
            for dz in range(1, NZ):
                remote(mbuf.at[z], mbuf.at[z], msem.at[dz], dev(dz=dz))
        if s > 1:
            xy_direct(s - 1)
        if s == 2:
            other = 1 - c
            arrived(toks.at[other], psem.at[1])
            arrived(cots.at[other], psem.at[2])
            multiply(0, first=True)
        if s > 3:
            finish(s - 3)
    xy_direct(8)
    for s in (6, 7, 8):
        finish(s)

    hc = pl.ds(al(c * HR, HR), HR)
    ho = pl.ds(al(o * HR, HR), HR)
    xpb[0, :, hc] = accx[:, B0 : B0 + HR].astype(BF)
    xpb[1, :, hc] = accy[:, 0:HR].astype(BF)
    remote(xpb.at[:, :, hc], xpb.at[:, :, hc], psem.at[5], partner)
    gate = accx[:, G0 : G0 + HF]
    up = accx[:, U0 : U0 + HF]
    dhid = accy[:, HR : HR + HF]
    sig = jax.nn.sigmoid(gate)
    silu = gate * sig
    hid[...] = (silu * up).astype(BF)
    dgu[:, 0:HF] = (dhid * up * sig * (1.0 + gate * (1.0 - sig))).astype(BF)
    dgu[:, HF : 2 * HF] = (dhid * silu).astype(BF)
    arrived(xpb.at[:, :, ho], psem.at[5])

    over_rows = (((0,), (0,)), ((), ()))
    l01 = lax.dot_general(xpb[0], dgu[...], over_rows, preferred_element_type=F32)
    lsend[0] = l01[:, 0:HF].astype(BF)
    lsend[1] = l01[:, HF : 2 * HF].astype(BF)
    lsend[2] = lax.dot_general(xpb[1], hid[...], over_rows, preferred_element_type=F32).astype(BF)

    plane = [(dx, dy) for dy in range(NY) for dx in range(NX) if (dx, dy) != (0, 0)]
    far_first = sorted(plane, key=lambda t: -(min(t[0], NX - t[0]) + min(t[1], NY - t[1])))

    def back(dx, dy):
        return ((-dy) % NY) * NX + (-dx) % NX

    def part_of(dx, dy):
        return lax.rem(y + dy, NY) * NX + lax.rem(x + dx, NX)

    def rows_of(q):
        return pl.ds(al(q * NZ, NZ), NZ)

    for dx, dy in far_first:
        q = part_of(dx, dy)
        remote(lsend.at[:, rows_of(q)], lrecv.at[p], rsem.at[back(dx, dy)], dev(dx=dx, dy=dy))
    lrecv[p] = lsend[:, rows_of(p)]

    def dx_of(core, out):
        rows = pl.ds(al(core * TOK, TOK), TOK)
        lhs = dgu[rows, :]

        @pl.loop(0, NZ)
        def _(i):
            out[:, pl.ds(al(i * 128, 128), 128)] = lax.dot_general(
                lhs, wbuf[i, :, 0 : 2 * HF], (((1,), (1,)), ((), ())), preferred_element_type=F32
            )

    dx_of(o, dxp)
    remote(dxp, dxr, psem.at[6], partner)

    def sum_parts(own, bufs):
        total = own
        for b in bufs:
            total = total + b.astype(F32)
        return total

    for dx, dy in plane:
        arrived(lrecv.at[part_of(dx, dy)], rsem.at[dy * NX + dx])
    total = lrecv[0].astype(F32)
    for q in range(1, NP):
        total = total + lrecv[q].astype(F32)
    t0b[...] = total.astype(BF)
    for i, dz in enumerate((1, -1, -2)):
        remote(t0b, nearb.at[i], nsem.at[i], dev(dz=dz))
    for i in range(3):
        arrived(nearb.at[i], nsem.at[i])
    total = sum_parts(total, [nearb[i] for i in range(3)])
    t1b[...] = total.astype(BF)
    for i, dz in ((2, 8), (0, 4), (1, -4)):
        remote(t1b, farb.at[i], fsem.at[i], dev(dz=dz))

    rows = pl.ds(al(c * TOK, TOK), TOK)
    arrived(dxr, psem.at[6])
    lhs_own = dgu[rows, :]

    @pl.loop(0, NZ)
    def _(i):
        cols = pl.ds(al(i * 128, 128), 128)
        part = lax.dot_general(
            lhs_own, wbuf[i, :, 0 : 2 * HF], (((1,), (1,)), ((), ())), preferred_element_type=F32
        )
        dxo[:, cols] = (part + dxr[:, cols]).astype(BF)

    outs = []

    def store(src, dst):
        cp = pltpu.make_async_copy(src, dst, lsem.at[8 + len(outs)])
        cp.start()
        outs.append(cp)

    store(dxo, dx_hbm)

    for i in range(3):
        arrived(farb.at[i], fsem.at[i])
    total = sum_parts(total, [farb[i] for i in range(3)])

    sq = jnp.sum(jnp.sum(total * total, axis=0), axis=0, keepdims=True)
    sq = jnp.sum(sq, axis=1, keepdims=True)
    sqo[...] = jnp.broadcast_to(sq, (1, HF))
    remote(sqo, sqp, psem.at[7], partner)
    zrow = lax.broadcasted_iota(jnp.int32, (3, NZ, HF), 1) == z
    mine3 = jnp.sum(jnp.where(zrow, total, 0.0), axis=1)
    lrow[0:3, :] = mine3
    lrow[3:8, :] = jnp.zeros((5, HF), F32)
    arrived(sqp, psem.at[7])
    sqb[p] = sqo[...] + sqp[...]
    for dx, dy in far_first:
        remote(sqb.at[p], sqb.at[p], qsem.at[back(dx, dy)], dev(dx=dx, dy=dy))
    lall[p] = lrow[...]
    for dx, dy in far_first:
        remote(lrow, lall.at[p], rowsem.at[back(dx, dy)], dev(dx=dx, dy=dy))
    for dz in range(1, NZ):
        arrived(mbuf.at[origin(dz)], msem.at[dz])
    for dx, dy in plane:
        arrived(sqb.at[part_of(dx, dy)], qsem.at[dy * NX + dx])
    ssum = sqb[0]
    for q in range(1, NP):
        ssum = ssum + sqb[q]
    factor = jnp.minimum(1.0, EPS_LIMIT / jnp.sqrt(ssum + 1e-06))

    def adam(low, first, second):
        grad = factor * low
        nf = 0.5 * first + 0.5 * grad
        ns = 0.9 * second + 0.1 * grad * grad
        return nf, ns

    for k in range(3):
        nf, ns = adam(total[k], mbuf[:, k, :], mbuf[:, 3 + k, :])
        sbuf[k, rows_of(p), :] = (nf / (jnp.sqrt(ns) + 1e-08)).astype(BF)
    for dx, dy in far_first:
        mine = sbuf.at[:, rows_of(p)]
        remote(mine, mine, stsem.at[back(dx, dy)], dev(dx=dx, dy=dy))

    for dx, dy in plane:
        arrived(lall.at[part_of(dx, dy)], rowsem.at[dy * NX + dx])
    remote(lall.at[pl.ds(al(o * 8, 8), 8)], loth, psem.at[8], partner)
    fc = pl.ds(al(c * HF, HF), HF)
    fo = pl.ds(al(o * HF, HF), HF)
    for k in range(3):
        nf, ns = adam(lall[pl.ds(al(c * 8, 8), 8), k, :], fmv[k, :, fc], smv[k, :, fc])
        nfv[k, :, fc] = nf
        nsv[k, :, fc] = ns
    arrived(loth, psem.at[8])
    for k in range(3):
        nf, ns = adam(loth[:, k, :], fmv[k, :, fo], smv[k, :, fo])
        nfv[k, :, fo] = nf
        nsv[k, :, fo] = ns
    store(nfv, nf_hbm)
    store(nsv, ns_hbm)

    arrived(bp.at[o], psem.at[3])
    for dx, dy in plane:
        arrived(sbuf.at[:, rows_of(part_of(dx, dy))], stsem.at[dy * NX + dx])

    def update(core, k):
        st = sbuf[k]
        return jnp.dot(bp[core, 0], st, preferred_element_type=F32) + jnp.dot(
            bp[core, 1], st, preferred_element_type=F32
        )

    for k in range(3):
        uov[k] = update(o, k)
    remote(uov, up_hbm.at[:, :, fc], psem.at[9], partner)
    for k in range(3):
        ucv[k] = update(c, k)
    store(ucv, up_hbm.at[:, :, fc])
    arrived(up_hbm.at[:, :, fo], psem.at[9])
    for cp in outs:
        cp.wait()
    for cp in sends:
        cp.wait_send()


def local(tokens, cotangent, w_gate, w_up, w_down, basis, first_moment, second_moment):
    anywhere = pl.BlockSpec(memory_space=pl.ANY)
    dma = pltpu.SemaphoreType.DMA
    v = pltpu.VMEM
    part = (3, NZ, HF)
    scratch = [
        v((2, TOK, D), BF), v((2, TOK, D), BF), v((NZ, 128, PW), BF),
        v((ROWS, FF), BF), v((ROWS, FF), BF), v((ROWS, FF), BF), v((ROWS, RANK), F32),
        v((3, 8, FF), F32), v((3, 8, FF), F32),
        v((ROWS, PW), BF), v((2, 2, ROWS, RANK), BF),
        v((8, HF), F32), v((8, HF), F32), v((NZ, 8, HF), F32),
        v((2 * TOK, D0), F32), v((2 * TOK, HR + HF), F32),
        v((2, 2 * TOK, RANK), BF), v((2 * TOK, 2 * HF), BF), v((2 * TOK, HF), BF),
        v((3, RANK, HF), BF), v((NP, *part), BF),
        v((TOK, D), F32), v((TOK, D), F32), v((TOK, D), BF),
        v(part, BF), v((3, *part), BF), v(part, BF), v((3, *part), BF),
        v((1, HF), F32), v((1, HF), F32), v((NP, 1, HF), F32),
        v((8, HF), F32), v((NP, 8, HF), F32), v((8, 8, HF), F32),
        v((3, RANK, HF), BF), v((3, ROWS, HF), F32), v((3, ROWS, HF), F32),
        v((3, 8, FF), F32), v((3, 8, FF), F32),
        dma((12,)), dma((NSEND,)), dma((2, NZ)), dma((2, 3, NZ)), dma((10,)),
        dma((NZ,)), dma((NP,)), dma((3,)), dma((3,)), dma((NP,)), dma((NP,)), dma((NP,)),
    ]
    return pl.pallas_call(
        kernel,
        out_shape=(
            jax.ShapeDtypeStruct((TOK, D), BF),
            jax.ShapeDtypeStruct((3, 8, FF), F32),
            jax.ShapeDtypeStruct((3, 8, FF), F32),
            jax.ShapeDtypeStruct((3, ROWS, FF), F32),
        ),
        in_specs=[anywhere] * 8,
        out_specs=(anywhere,) * 4,
        scratch_shapes=scratch,
        compiler_params=pltpu.CompilerParams(
            collective_id=0, has_side_effects=True, vmem_limit_bytes=60 * 1024 * 1024
        ),
    )(tokens, cotangent, w_gate, w_up, w_down, basis, first_moment, second_moment)


def solution(mesh):
    both = ("group", "member")
    placed = (
        P(both, None), P(both, None), P("member", None), P("member", None), P("member", None),
        P("member", None), P(None, "member", None), P(None, "member", None),
    )
    return jax.shard_map(
        local,
        mesh=mesh,
        in_specs=placed,
        out_specs=(P(both, None), P(None, "member", None), P(None, "member", None), P(None, "member", None)),
        check_vma=False,
    )
```

time: 338 us -> 89 us (0.26)
  blocking collectives: 254 us -> 0 us
  Pallas kernels: 0 us -> 84 us
  waiting for transfers between devices: 32.3 us -> 0 us
  matrix products: 15.2 us -> 0 us
  between operations: 14.9 us -> 0.66 us
  starting transfers between devices: 12.3 us -> 0 us
  other arithmetic: 4.12 us -> 0 us
    all_to_all x2 -> x0, blocking collectives: 223 us -> none  [the longest x1 137 us: copy_for_each(): lax.all_to_all(jnp.broadcast_to(value[None], (peers, *value.shape)), axis...]
    pallas_call x0 -> x1, Pallas kernels: none -> 84 us  [local(): pl.pallas_call(kernel, out_shape=(jax.ShapeDtypeStruct((TOK, D), BF), jax...]
    all_gather x2 -> x0, blocking collectives: 31.4 us -> none  [gather_in_order(): pieces = lax.all_gather(pieces, axes[k], axis=0, tiled=True)]
    all_to_all x2 -> x0, waiting for transfers between devices: 19.6 us -> none  [copy_for_each(): lax.all_to_all(jnp.broadcast_to(value[None], (peers, *value.shape)), axis...]
    dot_general x16 -> x0, matrix products: 15.2 us -> none  [the longest x2 5.62 us: contract_cols(): lax.dot_general(left, right, (((1,), (1,)), ((), ())), preferred_element_...]
    all_gather x1 -> x0, waiting for transfers between devices: 12.7 us -> none  [in_one_piece(): lax.all_gather(both, axis, axis=dim, tiled=True)]
    all_to_all x2 -> x0, starting transfers between devices: 12.3 us -> none  [copy_for_each(): lax.all_to_all(jnp.broadcast_to(value[None], (peers, *value.shape)), axis...]
  transfers between devices with their start and end apart: 3 -> 0, of which waited for: 3 -> 0; matrix products, arithmetic and copies ran while one was open for 2% -> 0% of each run, Pallas kernels for 0% -> 0%
where the time goes in v1:
time: 89 us; the launch traced here: 88.8 us
  Pallas kernels  84 us (94%)
  local copies, waits for them, and re-layouts  4.12 us (5%)
    pallas_call x1, Pallas kernels, local(): pl.pallas_call(kernel, out_shape=(jax.ShapeDtypeStruct((TOK, D), BF), jax...  84 us
    unnamed x10, local copies, waits for them, and re-layouts  4.12 us

profile of v1, /device:TPU:1, one launch (start us, length us, event | category | flops | bytes accessed | tf_op | source)
XLA Modules:
  0.0 88.8 jit_solution(6154089630195850169)
XLA Ops:
  0.6 84.0 %shard_map.111 = (bf16[128,2048]{1,0:T(8,128)(2,1)}, f32[3,8,512]{2,1,0:T(8,128)}, f32[3,8,512]{2,1,0:T(8,128)}, f32[3,64,512]{2,1,0:T(8,128)}) custom-call(bf16[128,2048]{1,0:T(8,128)(2,1)} %tok_hbm.1, bf16[128,2048]{1,0:T(8,128)(2,1)} %cot_hbm.1, bf16[64,512]{1,0:T(8,128)(2,1)} %wg_hbm.1, bf16[64,512]{1,0:T(8,128)(2,1)} %wu_hbm.1, bf16[64,512]{1,0:T(8,128)(2,1)} %wd_hbm.1, ...), custom_call_target="tpu_custom_call" | custom-call | tf_op jit(solution)/shard_map/pallas_call | solution.py:459
  84.6 0.0 copy-start.2
  84.6 0.0 copy-start
  84.6 1.9 %copy.16 = bf16[128,2048]{1,0:T(8,128)(2,1)} copy(bf16[128,2048]{1,0:T(8,128)(2,1)} %get-tuple-element.8) | data formatting | bytes 1048576
  86.6 0.0 copy-done.2
  86.6 0.0 copy-start.1
  86.6 0.6 copy.17
  87.2 0.2 copy-done.1
  87.4 0.6 copy.18
  88.0 0.0 copy-done
  88.0 0.7 copy.19
Async XLA Ops:
  84.6 2.0 %copy-start.2 = (f32[3,8,512]{2,1,0:T(8,128)S(1)}, f32[3,8,512]{2,1,0:T(8,128)}, u32[]{:S(2)}) copy-start(f32[3,8,512]{2,1,0:T(8,128)} %get-tuple-element.9) | copy-start | bytes 147460
  84.6 3.4 %copy-start = (f32[3,64,512]{2,1,0:T(8,128)S(1)}, f32[3,64,512]{2,1,0:T(8,128)}, u32[]{:S(2)}) copy-start(f32[3,64,512]{2,1,0:T(8,128)} %get-tuple-element.11) | copy-start | bytes 1179652
  86.6 0.8 copy-start.1

commit v2 on v1

--- a/solution.py
+++ b/solution.py
@@ -38,6 +38,9 @@
 
 
 NSEND = 240
+
+PLAN = {0: (2, 1), 2: (4, 3), 4: (6, 5), 6: (8, 7)}
+DIRECT = (7, 8)
 
 
 def kernel(
@@ -79,7 +82,7 @@
 
     barrier = pltpu.get_barrier_semaphore()
     near = [partner]
-    near += [dev(dz=1), dev(dz=-1), dev(dz=2), dev(dz=-2)]
+    near += [dev(dz=e * t) for t in PLAN[0] for e in (1, -1)]
     near += [dev(dx=1), dev(dx=-1), dev(dx=2)]
     near += [dev(dy=1), dev(dy=-1), dev(dy=2)]
     for d in near:
@@ -149,8 +152,9 @@
     for h, off in ((c, own_off), (o, oth_off)):
         if h is o:
             arrived(wbuf.at[z, pl.ds(al(o * ROWS, ROWS), ROWS)], psem.at[0])
-        for dz in (1, -1, 2, -2):
-            zsend(z, h, off, dz, dz % NZ)
+        for t in PLAN[0]:
+            zsend(z, h, off, t, t)
+            zsend(z, h, off, -t, NZ - t)
 
     for cp in ld_t:
         cp.wait()
@@ -179,17 +183,22 @@
             rel = s if d == 0 else NZ - s
             zo = origin(rel)
             sgn = 1 if d == 0 else -1
-            hs = (0, 1) if s < 8 else ((0,) if d == 0 else (1,))
+            hs = (0, 1) if s < 8 else (d,)
+            later = PLAN.get(s, ())
             for h in hs:
                 arrived(zchunk(zo, roff(h)), zsem.at[h, rel])
-                if s % 2 == 0 and s < 8:
-                    zsend(zo, h, roff(h), sgn, (rel + sgn) % NZ)
-                    if s + 2 < 8 or (d == 0) == (h == 0):
-                        zsend(zo, h, roff(h), 2 * sgn, (rel + 2 * sgn) % NZ)
+                for t in later[:1]:
+                    if t < 8 or h == d:
+                        zsend(zo, h, roff(h), sgn * (t - s), (rel + sgn * (t - s)) % NZ)
             for h in hs:
-                for e in (1, -1):
+                for t in later[1:]:
+                    if t < 8 or h == d:
+                        zsend(zo, h, roff(h), sgn * (t - s), (rel + sgn * (t - s)) % NZ)
+            for h in hs:
+                for e in (2, 1, -1) if s in DIRECT else (1, -1):
                     t = dev(dx=e) if h == 0 else dev(dy=e)
-                    remote(zchunk(zo, roff(h)), zchunk(zo, roff(h)), xysem.at[h, 0 if e == 1 else 1, rel], t)
+                    way = {1: 0, -1: 1, 2: 2}[e]
+                    remote(zchunk(zo, roff(h)), zchunk(zo, roff(h)), xysem.at[h, way, rel], t)
 
     def pieces(s):
         if s == 8:
@@ -207,8 +216,9 @@
                 e = -1 if way == 0 else 1
                 ch = zchunk(zo, step_of(h, e))
                 arrived(ch, xysem.at[h, way, rel])
-                t = dev(dx=-e) if h == 0 else dev(dy=-e)
-                remote(ch, ch, xysem.at[h, 2, rel], t)
+                if s not in DIRECT:
+                    t = dev(dx=-e) if h == 0 else dev(dy=-e)
+                    remote(ch, ch, xysem.at[h, 2, rel], t)
 
     def xy_rest(s):
         for rel, ways in pieces(s):
@@ -240,7 +250,7 @@
 
     for s in range(1, 9):
         z_arrive(s)
-        if s == 6:
+        if s == 8:
             arrived(mrecv, psem.at[4])
             mine = pcore == c
             mbuf[z] = jnp.where(mine, mbuf[z], mrecv[...])

time: 89 us -> 84.6 us (0.951)
  Pallas kernels: 84 us -> 79.6 us
    pallas_call x1, Pallas kernels: 84 us -> 79.6 us  [local(): pl.pallas_call(kernel, out_shape=(jax.ShapeDtypeStruct((TOK, D), BF), jax...]
where the time goes in v2:
time: 84.6 us; the launch traced here: 84.4 us
  Pallas kernels  79.6 us (94%)
  local copies, waits for them, and re-layouts  4.12 us (5%)
    pallas_call x1, Pallas kernels, local(): pl.pallas_call(kernel, out_shape=(jax.ShapeDtypeStruct((TOK, D), BF), jax...  79.6 us
    unnamed x10, local copies, waits for them, and re-layouts  4.12 us

profile of v2, /device:TPU:1, one launch (start us, length us, event | category | flops | bytes accessed | tf_op | source)
XLA Modules:
  0.0 84.4 jit_solution(8642645900511430106)
XLA Ops:
  0.6 79.6 %shard_map.111 = (bf16[128,2048]{1,0:T(8,128)(2,1)}, f32[3,8,512]{2,1,0:T(8,128)}, f32[3,8,512]{2,1,0:T(8,128)}, f32[3,64,512]{2,1,0:T(8,128)}) custom-call(bf16[128,2048]{1,0:T(8,128)(2,1)} %tok_hbm.1, bf16[128,2048]{1,0:T(8,128)(2,1)} %cot_hbm.1, bf16[64,512]{1,0:T(8,128)(2,1)} %wg_hbm.1, bf16[64,512]{1,0:T(8,128)(2,1)} %wu_hbm.1, bf16[64,512]{1,0:T(8,128)(2,1)} %wd_hbm.1, ...), custom_call_target="tpu_custom_call" | custom-call | tf_op jit(solution)/shard_map/pallas_call | solution.py:469
  80.2 0.0 copy-start.2
  80.2 0.0 copy-start
  80.3 1.9 %copy.16 = bf16[128,2048]{1,0:T(8,128)(2,1)} copy(bf16[128,2048]{1,0:T(8,128)(2,1)} %get-tuple-element.8) | data formatting | bytes 1048576
  82.2 0.0 copy-done.2
  82.2 0.0 copy-start.1
  82.2 0.6 copy.17
  82.8 0.2 copy-done.1
  83.0 0.6 copy.18
  83.6 0.0 copy-done
  83.6 0.7 copy.19
Async XLA Ops:
  80.2 2.0 %copy-start.2 = (f32[3,8,512]{2,1,0:T(8,128)S(1)}, f32[3,8,512]{2,1,0:T(8,128)}, u32[]{:S(2)}) copy-start(f32[3,8,512]{2,1,0:T(8,128)} %get-tuple-element.9) | copy-start | bytes 147460
  80.2 3.4 %copy-start = (f32[3,64,512]{2,1,0:T(8,128)S(1)}, f32[3,64,512]{2,1,0:T(8,128)}, u32[]{:S(2)}) copy-start(f32[3,64,512]{2,1,0:T(8,128)} %get-tuple-element.11) | copy-start | bytes 1179652
  82.2 0.8 copy-start.1

commit v3 on v2

v3 whole, which is shorter than its diff:
```python
import functools
import math

import jax
import jax.numpy as jnp
from jax import lax
from jax.experimental import pallas as pl
from jax.experimental.pallas import tpu as pltpu
from jax.sharding import PartitionSpec as P

BF = jnp.bfloat16
F32 = jnp.float32
MESH = pl.DeviceIdType.MESH

D = 2048
FF = 512
RANK = 256
TOK = 128
NX, NY, NZ = 4, 4, 16
NP = NX * NY
HF = FF // 2
HR = RANK // 2
ROWS = 64
PW = 3 * HF + HR
EPS_LIMIT = math.sqrt(3.0 * RANK * FF)

G0, U0, B0, D0 = 0, HF, 2 * HF, 2 * HF + HR


class Pool:
    def __init__(self, ref, count, near):
        self.ref, self.count, self.near, self.started, self.done = ref, count, near, [], 0

    def start(self, src, dst, recv, device, like=None):
        if len(self.started) - self.done == self.count:
            self.wait_oldest(recv)
        pltpu.make_async_remote_copy(
            src_ref=src, dst_ref=dst, send_sem=self.ref.at[len(self.started) % self.count],
            recv_sem=recv, device_id=device, device_id_type=MESH,
        ).start()
        self.started.append(src if like is None else like)

    def wait_oldest(self, recv):
        like = self.started[self.done]
        like = like() if callable(like) else like
        pltpu.make_async_remote_copy(
            src_ref=like, dst_ref=like, send_sem=self.ref.at[self.done % self.count],
            recv_sem=recv, device_id=self.near, device_id_type=MESH,
        ).wait_send()
        self.done += 1

    def drain(self):
        while self.done < len(self.started):
            self.wait_oldest(self.ref.at[0])


NLEAD, NBOTH, NHELP, NGATHER = 72, 24, 8, 160

PLAN = {0: (2, 1), 2: (4, 3), 4: (6, 5), 6: (8, 7)}
DIRECT = (7, 8)


def kernel(
    tok_hbm, cot_hbm, wg_hbm, wu_hbm, wd_hbm, bas_hbm, fm_hbm, sm_hbm,
    dxo, nfv, nsv, upv,
    toks, cots, wbuf, wgv, wuv, wdv, basv, fmv, smv,
    pk, bp, msend, mrecv, mbuf,
    accx, accy, xpb, dgu, hid, lsend, lrecv,
    dxp, dxr, tv, t0b, nearb, t1b, farb,
    sqb, sfac, lrow, lall, loth, sbuf, uov,
    lsem, lead_sem, both_sem, help_sem, gather_sem, zsem, xysem, psem, msem, rsem, nsem, fsem, qsem, rowsem, stsem,
):
    g = lax.axis_index("group")
    m = lax.axis_index("member")
    y, x = lax.div(g, NX), lax.rem(g, NX)
    z, c = lax.div(m, 2), lax.rem(m, 2)
    o = 1 - c
    p = g
    leads, helps = c == 1, c == 0

    xs = [x] + [lax.rem(x + d, NX) for d in range(1, NX)]
    ys = [y] + [lax.rem(y + d, NY) for d in range(1, NY)]
    zs = [z] + [lax.rem(z + d, NZ) for d in range(1, NZ)]
    groups = {(i, j): ys[j] * NX + xs[i] for i in range(NX) for j in range(NY)}
    groups[0, 0] = g
    members = [zs[i] * 2 + c for i in range(NZ)]
    leaders = [zs[i] * 2 + 1 for i in range(NZ)]
    xrows = [16 * xs[i] for i in range(NX)]
    yrows = [64 + 16 * ys[i] for i in range(NY)]

    def dev(dx=0, dy=0, dz=0, lead=False):
        return (groups[dx % NX, dy % NY], (leaders if lead else members)[dz % NZ])

    partner = (g, z * 2 + o)

    local = []

    def load(src, dst):
        cp = pltpu.make_async_copy(src, dst, lsem.at[len(local)])
        cp.start()
        local.append(cp)
        return cp

    ld_w = [load(wg_hbm, wgv), load(wu_hbm, wuv), load(wd_hbm, wdv), load(bas_hbm, basv)]
    ld_t = [load(tok_hbm, toks.at[c]), load(cot_hbm, cots.at[c])]
    ld_m = [load(fm_hbm, fmv), load(sm_hbm, smv)]

    barrier = pltpu.get_barrier_semaphore()
    near = [partner, dev(dx=1), dev(dx=-1), dev(dx=2), dev(dy=1), dev(dy=-1), dev(dy=2)]
    near += [dev(dz=e * t) for t in PLAN[0] for e in (1, -1)]

    for d in near:
        pl.semaphore_signal(barrier, inc=1, device_id=d, device_id_type=MESH)

    lead = Pool(lead_sem, NLEAD, partner)
    both = Pool(both_sem, NBOTH, partner)
    helper = Pool(help_sem, NHELP, partner)
    gather = Pool(gather_sem, NGATHER, partner)

    def chunk():
        return wbuf.at[0, pl.ds(0, 16)]

    def part():
        return lsend.at[:, pl.ds(0, NZ)]


    def arrived(dst, recv):
        pltpu.make_async_remote_copy(
            src_ref=dst, dst_ref=dst, send_sem=both_sem.at[0], recv_sem=recv,
            device_id=partner, device_id_type=MESH,
        ).wait_recv()

    def al(v, n):
        return pl.multiple_of(v, n)

    def roff(h, e=0):
        return al(xrows[e % NX] if h == 0 else yrows[e % NY], 16)

    for cp in ld_w:
        cp.wait()
    pr = lax.broadcasted_iota(jnp.int32, (RANK, RANK), 0)
    pc = lax.broadcasted_iota(jnp.int32, (RANK, RANK), 1)
    perm = (pr == (pc & (NZ - 1)) * NP + (pc >> 4)).astype(F32).astype(BF)
    bas = basv[...]
    bh = bas.astype(BF)
    bl = (bas - bh.astype(F32)).astype(BF)
    bp[c, 0] = jnp.dot(bh, perm, preferred_element_type=F32).astype(BF)
    bp[c, 1] = jnp.dot(bl, perm, preferred_element_type=F32).astype(BF)
    own_rows = pl.ds(al(c * ROWS, ROWS), ROWS)
    for half, put in ((o, "partner"), (c, "own")):
        fs = pl.ds(al(half * HF, HF), HF)
        rs = pl.ds(al(half * HR, HR), HR)
        for col, width, val in (
            (G0, HF, wgv[:, fs]), (U0, HF, wuv[:, fs]), (B0, HR, bp[c, 0, :, rs]), (D0, HF, wdv[:, fs]),
        ):
            if put == "partner":
                pk[:, col : col + width] = val
            else:
                wbuf[z, own_rows, col : col + width] = val

    pl.semaphore_wait(barrier, len(near))

    both.start(pk, wbuf.at[z, own_rows], psem.at[0], partner)

    def held(zo, row):
        return wbuf.at[zo, pl.ds(row, 16)]

    def zsend(zo, h, row, dz, rel):
        gather.start(held(zo, row), held(zo, row), zsem.at[h, rel], dev(dz=dz), chunk)

    own_off = al((1 - c) * xrows[0] + c * yrows[0], 16)
    oth_off = al(c * xrows[0] + (1 - c) * yrows[0], 16)
    for h, off in ((c, own_off), (o, oth_off)):
        if h is o:
            arrived(wbuf.at[z, pl.ds(al(o * ROWS, ROWS), ROWS)], psem.at[0])
        for t in PLAN[0]:
            zsend(z, h, off, t, t)
            zsend(z, h, off, -t, NZ - t)

    for cp in ld_t:
        cp.wait()
    both.start(toks.at[c], toks.at[c], psem.at[1], partner)
    both.start(cots.at[c], cots.at[c], psem.at[2], partner)

    for cp in ld_m:
        cp.wait()
    prow = lax.rem(p, 8)
    pcore = lax.div(p, 8)
    msend[6:8, :] = jnp.zeros((2, FF), F32)
    for i, mv in enumerate((fmv, smv)):
        for k in range(3):
            msend[3 * i + k : 3 * i + k + 1, :] = mv[k, pl.ds(prow, 1), :]

    @pl.when(helps)
    def _():
        helper.start(bp.at[0], bp.at[0], psem.at[3], partner, lambda: bp.at[0])
        helper.start(msend, mrecv, psem.at[4], partner)

    def origin(rel):
        return zs[-rel % NZ]

    def aside(h, e):
        return dev(dx=e) if h == 0 else dev(dy=e)

    def z_arrive(s):
        for d in (0, 1):
            rel = s if d == 0 else NZ - s
            zo = origin(rel)
            sgn = 1 if d == 0 else -1
            hs = (0, 1) if s < 8 else (d,)
            later = PLAN.get(s, ())
            for h in hs:
                arrived(held(zo, roff(h)), zsem.at[h, rel])
                for t in later[:1]:
                    if t < 8 or h == d:
                        zsend(zo, h, roff(h), sgn * (t - s), (rel + sgn * (t - s)) % NZ)
            for h in hs:
                for t in later[1:]:
                    if t < 8 or h == d:
                        zsend(zo, h, roff(h), sgn * (t - s), (rel + sgn * (t - s)) % NZ)
            for h in hs:
                there = held(zo, roff(h))
                for e in (2, 1, -1) if s in DIRECT else (1, -1):
                    way = {1: 0, -1: 1, 2: 2}[e]
                    gather.start(there, there, xysem.at[h, way, rel], aside(h, e), chunk)

    def pieces(s):
        if s == 8:
            return [(8, (0, 1))]
        return [(s, (0, 0)), (NZ - s, (1, 1))]

    def xy_direct(s):
        for rel, ways in pieces(s):
            for h in (0, 1):
                e = -1 if ways[h] == 0 else 1
                ch = held(origin(rel), roff(h, e))
                arrived(ch, xysem.at[h, ways[h], rel])
                if s not in DIRECT:
                    gather.start(ch, ch, xysem.at[h, 2, rel], aside(h, -e), chunk)

    def xy_rest(s):
        for rel, ways in pieces(s):
            for h in (0, 1):
                way = 1 - ways[h]
                e = -1 if way == 0 else 1
                arrived(held(origin(rel), roff(h, e)), xysem.at[h, way, rel])
                arrived(held(origin(rel), roff(h, 2)), xysem.at[h, 2, rel])

    def multiply(rel, first=False):
        zo = origin(rel)
        cols = pl.ds(al(zo * 128, 128), 128)
        tk = toks[:, :, cols].reshape(2 * TOK, 128)
        ck = cots[:, :, cols].reshape(2 * TOK, 128)
        ax = jnp.dot(tk, wbuf[zo, :, 0:D0], preferred_element_type=F32)
        ay = jnp.dot(ck, wbuf[zo, :, B0:PW], preferred_element_type=F32)
        if first:
            accx[...] = ax
            accy[...] = ay
        else:
            accx[...] += ax
            accy[...] += ay

    def finish(s):
        xy_rest(s)
        for rel, _ in pieces(s):
            multiply(rel)

    for s in range(1, 9):
        z_arrive(s)
        if s > 1:
            xy_direct(s - 1)
        if s == 2:
            arrived(toks.at[o], psem.at[1])
            arrived(cots.at[o], psem.at[2])
            multiply(0, first=True)
        if s > 3:
            finish(s - 3)

    @pl.when(leads)
    def _():
        arrived(mrecv, psem.at[4])
        mbuf[z] = jnp.where(pcore == 1, msend[...], mrecv[...])
        for dz in range(1, NZ):
            lead.start(mbuf.at[z], mbuf.at[z], msem.at[dz], dev(dz=dz, lead=True), lambda: mbuf.at[0])

    xy_direct(8)
    for s in (6, 7, 8):
        finish(s)

    hc = pl.ds(al(c * HR, HR), HR)
    ho = pl.ds(al(o * HR, HR), HR)
    xpb[0, :, hc] = accx[:, B0 : B0 + HR].astype(BF)
    xpb[1, :, hc] = accy[:, 0:HR].astype(BF)
    both.start(xpb.at[:, :, hc], xpb.at[:, :, hc], psem.at[5], partner)
    gate = accx[:, G0 : G0 + HF]
    up = accx[:, U0 : U0 + HF]
    dhid = accy[:, HR : HR + HF]
    sig = jax.nn.sigmoid(gate)
    silu = gate * sig
    hid[...] = (silu * up).astype(BF)
    dgu[:, 0:HF] = (dhid * up * sig * (1.0 + gate * (1.0 - sig))).astype(BF)
    dgu[:, HF : 2 * HF] = (dhid * silu).astype(BF)
    arrived(xpb.at[:, :, ho], psem.at[5])

    over_rows = (((0,), (0,)), ((), ()))
    l01 = lax.dot_general(xpb[0], dgu[...], over_rows, preferred_element_type=F32)
    lsend[0] = l01[:, 0:HF].astype(BF)
    lsend[1] = l01[:, HF : 2 * HF].astype(BF)
    lsend[2] = lax.dot_general(xpb[1], hid[...], over_rows, preferred_element_type=F32).astype(BF)

    plane = [(dx, dy) for dy in range(NY) for dx in range(NX) if (dx, dy) != (0, 0)]
    far_first = sorted(plane, key=lambda t: -(min(t[0], NX - t[0]) + min(t[1], NY - t[1])))

    def back(dx, dy):
        return ((-dy) % NY) * NX + (-dx) % NX

    def part_of(dx, dy):
        return groups[dx, dy]

    def rows_of(q):
        return pl.ds(al(q * NZ, NZ), NZ)

    for dx, dy in far_first:
        q = part_of(dx, dy)
        both.start(lsend.at[:, rows_of(q)], lrecv.at[p, c], rsem.at[c, back(dx, dy)], dev(dx=dx, dy=dy, lead=True), part)

    @pl.when(leads)
    def _():
        lrecv[p, 1] = lsend[:, rows_of(p)]

    @pl.when(helps)
    def _():
        helper.start(lsend.at[:, rows_of(p)], lrecv.at[p, 0], rsem.at[0, 0], partner, part)

    def dx_part(core, put):
        lhs = dgu[pl.ds(al(core * TOK, TOK), TOK), :]

        @pl.loop(0, NZ)
        def _(i):
            put(pl.ds(al(i * 128, 128), 128), lax.dot_general(
                lhs, wbuf[i, :, 0 : 2 * HF], (((1,), (1,)), ((), ())), preferred_element_type=F32
            ))

    def put_partner(cols, val):
        dxp[:, cols] = val

    def put_own(cols, val):
        dxo[:, cols] = (val + dxr[:, cols]).astype(BF)

    dx_part(o, put_partner)
    both.start(dxp, dxr, psem.at[6], partner)

    @pl.when(leads)
    def _():
        for half in (0, 1):
            for dx, dy in plane:
                arrived(lrecv.at[part_of(dx, dy), half], rsem.at[half, dy * NX + dx])
        arrived(lrecv.at[p, 0], rsem.at[0, 0])
        total = lrecv[0].astype(F32)
        for q in range(1, NP):
            total = total + lrecv[q].astype(F32)
        t0b[...] = total.astype(BF)
        for i, dz in enumerate((1, -1, -2)):
            lead.start(t0b, nearb.at[i], nsem.at[i], dev(dz=dz, lead=True))
        for i in range(3):
            arrived(nearb.at[i], nsem.at[i])
        for i in range(3):
            total = total + nearb[i].astype(F32)
        t1b[...] = total.astype(BF)
        for i, dz in ((2, 8), (0, 4), (1, -4)):
            lead.start(t1b, farb.at[i], fsem.at[i], dev(dz=dz, lead=True))
        tv[...] = total

    arrived(dxr, psem.at[6])
    dx_part(c, put_own)
    def adam(low, first, second, factor):
        grad = factor * low
        nf = 0.5 * first + 0.5 * grad
        ns = 0.9 * second + 0.1 * grad * grad
        return nf, ns

    def factor_of(ssum):
        return jnp.minimum(1.0, EPS_LIMIT / jnp.sqrt(ssum + 1e-06))

    halves = (slice(0, HF), slice(HF, FF))

    def moments(low):
        factor = factor_of(sfac[0:1, :])
        for k in range(3):
            nf, ns = adam(low(k), fmv[k], smv[k], jnp.concatenate([factor, factor], axis=1))
            nfv[k] = nf
            nsv[k] = ns

    @pl.when(leads)
    def _():
        for i in range(3):
            arrived(farb.at[i], fsem.at[i])
        total = tv[...]
        for i in range(3):
            total = total + farb[i].astype(F32)
        flat = total.reshape(6 * NZ, HF)
        sq = jnp.sum(jnp.sum(flat * flat, axis=0, keepdims=True), axis=1, keepdims=True)
        sqb[p] = jnp.broadcast_to(sq, (1, HF))
        for dx, dy in far_first:
            lead.start(sqb.at[p], sqb.at[p], qsem.at[back(dx, dy)], dev(dx=dx, dy=dy, lead=True), lambda: sqb.at[0])
        zrow = lax.broadcasted_iota(jnp.int32, (3, NZ, HF), 1) == z
        lrow[3:8, :] = jnp.zeros((5, FF), F32)
        for half in (0, 1):
            lrow[0:3, halves[half]] = jnp.sum(jnp.where(zrow, total[half], 0.0), axis=1)
        lall[p] = lrow[...]
        for dx, dy in far_first:
            lead.start(lrow, lall.at[p], rowsem.at[back(dx, dy)], dev(dx=dx, dy=dy, lead=True))
        for dz in range(1, NZ):
            arrived(mbuf.at[origin(dz)], msem.at[dz])
        for dx, dy in plane:
            arrived(sqb.at[part_of(dx, dy)], qsem.at[dy * NX + dx])
        ssum = sqb[0]
        for q in range(1, NP):
            ssum = ssum + sqb[q]
        sfac[0:1, :] = ssum
        factor = factor_of(ssum)
        for k in range(3):
            for half in (0, 1):
                nf, ns = adam(total[half, k], mbuf[:, k, halves[half]], mbuf[:, 3 + k, halves[half]], factor)
                sbuf[k, rows_of(p), halves[half]] = (nf / (jnp.sqrt(ns) + 1e-08)).astype(BF)
        mine = sbuf.at[:, rows_of(p)]
        for dx, dy in far_first:
            lead.start(mine, mine, stsem.at[back(dx, dy)], dev(dx=dx, dy=dy, lead=True), lambda: sbuf.at[:, pl.ds(0, NZ)])
        for dx, dy in plane:
            arrived(lall.at[part_of(dx, dy)], rowsem.at[dy * NX + dx])
        lead.start(sfac, sfac, psem.at[8], partner)
        lead.start(lall.at[0:8], loth, psem.at[10], partner, lambda: lall.at[0:8])
        moments(lambda k: lall[8:16, k, :])

    @pl.when(helps)
    def _():
        arrived(sfac, psem.at[8])
        arrived(loth, psem.at[10])
        moments(lambda k: loth[:, k, :])

    def update(core, k):
        st = sbuf[k]
        return jnp.dot(bp[core, 0], st, preferred_element_type=F32) + jnp.dot(
            bp[core, 1], st, preferred_element_type=F32
        )

    @pl.when(leads)
    def _():
        arrived(bp.at[0], psem.at[3])
        for dx, dy in plane:
            arrived(sbuf.at[:, rows_of(part_of(dx, dy))], stsem.at[dy * NX + dx])
        for k in range(3):
            uov[k] = update(0, k)
        lead.start(uov, upv, psem.at[9], partner)
        for k in range(3):
            upv[k] = update(1, k)
        lead.drain()

    @pl.when(helps)
    def _():
        arrived(upv, psem.at[9])
        helper.drain()

    both.drain()
    gather.drain()


def local(tokens, cotangent, w_gate, w_up, w_down, basis, first_moment, second_moment):
    anywhere = pl.BlockSpec(memory_space=pl.ANY)
    dma = pltpu.SemaphoreType.DMA
    v = pltpu.VMEM
    part = (2, 3, NZ, HF)
    scratch = [
        v((2, TOK, D), BF), v((2, TOK, D), BF), v((NZ, 128, PW), BF),
        v((ROWS, FF), BF), v((ROWS, FF), BF), v((ROWS, FF), BF), v((ROWS, RANK), F32),
        v((3, 8, FF), F32), v((3, 8, FF), F32),
        v((ROWS, PW), BF), v((2, 2, ROWS, RANK), BF),
        v((8, FF), F32), v((8, FF), F32), v((NZ, 8, FF), F32),
        v((2 * TOK, D0), F32), v((2 * TOK, HR + HF), F32),
        v((2, 2 * TOK, RANK), BF), v((2 * TOK, 2 * HF), BF), v((2 * TOK, HF), BF),
        v((3, RANK, HF), BF), v((NP, *part), BF),
        v((TOK, D), F32), v((TOK, D), F32),
        v(part, F32), v(part, BF), v((3, *part), BF), v(part, BF), v((3, *part), BF),
        v((NP, 1, HF), F32), v((8, HF), F32),
        v((8, FF), F32), v((NP, 8, FF), F32), v((8, 8, FF), F32),
        v((3, RANK, FF), BF), v((3, ROWS, FF), F32),
        dma((8,)), dma((NLEAD,)), dma((NBOTH,)), dma((NHELP,)), dma((NGATHER,)), dma((2, NZ)), dma((2, 3, NZ)), dma((11,)),
        dma((NZ,)), dma((2, NP)), dma((3,)), dma((3,)), dma((NP,)), dma((NP,)), dma((NP,)),
    ]
    kept = [((TOK, D), BF), ((3, 8, FF), F32), ((3, 8, FF), F32), ((3, ROWS, FF), F32)]
    inside = pl.BlockSpec(memory_space=pltpu.VMEM)
    results = pl.pallas_call(
        kernel,
        out_shape=tuple(pltpu.VMEM(*k) for k in kept),
        in_specs=[anywhere] * 8,
        out_specs=(inside,) * 4,
        scratch_shapes=scratch,
        compiler_params=pltpu.CompilerParams(
            collective_id=0, has_side_effects=True, vmem_limit_bytes=58 * 1024 * 1024
        ),
    )(tokens, cotangent, w_gate, w_up, w_down, basis, first_moment, second_moment)
    return pl.pallas_call(
        put_out,
        out_shape=tuple(jax.ShapeDtypeStruct(*k) for k in kept),
        in_specs=[inside] * 4,
        out_specs=(anywhere,) * 4,
        scratch_shapes=[dma((4,))],
        compiler_params=pltpu.CompilerParams(vmem_limit_bytes=4 * 1024 * 1024),
    )(*results)


def put_out(a, b, c, d, a_hbm, b_hbm, c_hbm, d_hbm, sem):
    pairs = ((a, a_hbm), (b, b_hbm), (c, c_hbm), (d, d_hbm))
    copies = [pltpu.make_async_copy(src, dst, sem.at[i]) for i, (src, dst) in enumerate(pairs)]
    for cp in copies:
        cp.start()
    for cp in copies:
        cp.wait()


def solution(mesh):
    both = ("group", "member")
    placed = (
        P(both, None), P(both, None), P("member", None), P("member", None), P("member", None),
        P("member", None), P(None, "member", None), P(None, "member", None),
    )
    return jax.shard_map(
        local,
        mesh=mesh,
        in_specs=placed,
        out_specs=(P(both, None), P(None, "member", None), P(None, "member", None), P(None, "member", None)),
        check_vma=False,
    )
```

time: 84.6 us -> 79.6 us (0.941)
  local copies, waits for them, and re-layouts: 4.12 us -> 0 us
    unnamed x10 -> x0, local copies, waits for them, and re-layouts: 4.12 us -> none
    pallas_call x1 -> x2, Pallas kernels: 79.6 us -> 78.8 us  [the longest x1 77.8 us: local(): pl.pallas_call(kernel, out_shape=tuple((pltpu.VMEM(*k) for k in kept)), i...]
where the time goes in v3:
time: 79.6 us; the launch traced here: 79.5 us
  Pallas kernels  78.8 us (99%)
    pallas_call x1, Pallas kernels, local(): pl.pallas_call(kernel, out_shape=tuple((pltpu.VMEM(*k) for k in kept)), i...  77.8 us

profile of v3, /device:TPU:1, one launch (start us, length us, event | category | flops | bytes accessed | tf_op | source)
XLA Modules:
  0.0 79.5 jit_solution(10954748217412310379)
XLA Ops:
  0.6 77.8 %shard_map.111 = (bf16[128,2048]{1,0:T(8,128)(2,1)S(1)}, f32[3,8,512]{2,1,0:T(8,128)S(1)}, f32[3,8,512]{2,1,0:T(8,128)S(1)}, f32[3,64,512]{2,1,0:T(8,128)S(1)}) custom-call(bf16[128,2048]{1,0:T(8,128)(2,1)} %tok_hbm.1, bf16[128,2048]{1,0:T(8,128)(2,1)} %cot_hbm.1, bf16[64,512]{1,0:T(8,128)(2,1)} %wg_hbm.1, bf16[64,512]{1,0:T(8,128)(2,1)} %wu_hbm.1, ...), custom_call_target="tpu_custom_call" | custom-call | tf_op jit(solution)/shard_map/pallas_call | solution.py:492
  78.5 1.0 %shard_map.112 = (bf16[128,2048]{1,0:T(8,128)(2,1)}, f32[3,8,512]{2,1,0:T(8,128)}, f32[3,8,512]{2,1,0:T(8,128)}, f32[3,64,512]{2,1,0:T(8,128)}) custom-call(bf16[128,2048]{1,0:T(8,128)(2,1)S(1)} %get-tuple-element.8.a, f32[3,8,512]{2,1,0:T(8,128)S(1)} %get-tuple-element.9.b, f32[3,8,512]{2,1,0:T(8,128)S(1)} %get-tuple-element.10.c, ...), custom_call_target="tpu_custom_call" | custom-call | tf_op jit(solution)/shard_map/pallas_call | solution.py:502

commit v4 on v3

--- a/solution.py
+++ b/solution.py
@@ -68,7 +68,7 @@
     accx, accy, xpb, dgu, hid, lsend, lrecv,
     dxp, dxr, tv, t0b, nearb, t1b, farb,
     sqb, sfac, lrow, lall, loth, sbuf, uov,
-    lsem, lead_sem, both_sem, help_sem, gather_sem, zsem, xysem, psem, msem, rsem, nsem, fsem, qsem, rowsem, stsem,
+    lsem, lead_sem, both_sem, help_sem, gather_sem, part_sem, zsem, xysem, psem, msem, rsem, nsem, fsem, qsem, rowsem, stsem,
 ):
     g = lax.axis_index("group")
     m = lax.axis_index("member")
@@ -136,11 +136,11 @@
     def roff(h, e=0):
         return al(xrows[e % NX] if h == 0 else yrows[e % NY], 16)
 
-    for cp in ld_w:
-        cp.wait()
     pr = lax.broadcasted_iota(jnp.int32, (RANK, RANK), 0)
     pc = lax.broadcasted_iota(jnp.int32, (RANK, RANK), 1)
     perm = (pr == (pc & (NZ - 1)) * NP + (pc >> 4)).astype(F32).astype(BF)
+    for cp in ld_w:
+        cp.wait()
     bas = basv[...]
     bh = bas.astype(BF)
     bl = (bas - bh.astype(F32)).astype(BF)
@@ -203,23 +203,27 @@
         return dev(dx=e) if h == 0 else dev(dy=e)
 
     def z_arrive(s):
+        later = PLAN.get(s, ())
+        for h in (0, 1):
+            for d in (0, 1) if s < 8 else (h,):
+                rel = s if d == 0 else NZ - s
+                sgn = 1 if d == 0 else -1
+                arrived(held(origin(rel), roff(h)), zsem.at[h, rel])
+                for t in later[:1]:
+                    if t < 8 or h == d:
+                        zsend(origin(rel), h, roff(h), sgn * (t - s), (rel + sgn * (t - s)) % NZ)
+        for h in (0, 1):
+            for d in (0, 1):
+                rel = s if d == 0 else NZ - s
+                sgn = 1 if d == 0 else -1
+                for t in later[1:]:
+                    zsend(origin(rel), h, roff(h), sgn * (t - s), (rel + sgn * (t - s)) % NZ)
+
+    def xy_send(s):
         for d in (0, 1):
             rel = s if d == 0 else NZ - s
-            zo = origin(rel)
-            sgn = 1 if d == 0 else -1
-            hs = (0, 1) if s < 8 else (d,)
-            later = PLAN.get(s, ())
-            for h in hs:
-                arrived(held(zo, roff(h)), zsem.at[h, rel])
-                for t in later[:1]:
-                    if t < 8 or h == d:
-                        zsend(zo, h, roff(h), sgn * (t - s), (rel + sgn * (t - s)) % NZ)
-            for h in hs:
-                for t in later[1:]:
-                    if t < 8 or h == d:
-                        zsend(zo, h, roff(h), sgn * (t - s), (rel + sgn * (t - s)) % NZ)
-            for h in hs:
-                there = held(zo, roff(h))
+            for h in (0, 1) if s < 8 else (d,):
+                there = held(origin(rel), roff(h))
                 for e in (2, 1, -1) if s in DIRECT else (1, -1):
                     way = {1: 0, -1: 1, 2: 2}[e]
                     gather.start(there, there, xysem.at[h, way, rel], aside(h, e), chunk)
@@ -265,16 +269,21 @@
         for rel, _ in pieces(s):
             multiply(rel)
 
-    for s in range(1, 9):
-        z_arrive(s)
-        if s > 1:
-            xy_direct(s - 1)
-        if s == 2:
+    order = (2, 1, 4, 3, 6, 5, 8, 7)
+    for i in range(0, 8, 2):
+        for s in order[i : i + 2]:
+            z_arrive(s)
+            xy_send(s)
+        if i == 0:
             arrived(toks.at[o], psem.at[1])
             arrived(cots.at[o], psem.at[2])
             multiply(0, first=True)
-        if s > 3:
-            finish(s - 3)
+        else:
+            for s in order[i - 2 : i]:
+                xy_direct(s)
+        if i > 2:
+            for s in order[i - 4 : i - 2]:
+                finish(s)
 
     @pl.when(leads)
     def _():
@@ -283,8 +292,9 @@
         for dz in range(1, NZ):
             lead.start(mbuf.at[z], mbuf.at[z], msem.at[dz], dev(dz=dz, lead=True), lambda: mbuf.at[0])
 
-    xy_direct(8)
-    for s in (6, 7, 8):
+    for s in order[6:8]:
+        xy_direct(s)
+    for s in order[4:8]:
         finish(s)
 
     hc = pl.ds(al(c * HR, HR), HR)
@@ -300,14 +310,6 @@
     hid[...] = (silu * up).astype(BF)
     dgu[:, 0:HF] = (dhid * up * sig * (1.0 + gate * (1.0 - sig))).astype(BF)
     dgu[:, HF : 2 * HF] = (dhid * silu).astype(BF)
-    arrived(xpb.at[:, :, ho], psem.at[5])
-
-    over_rows = (((0,), (0,)), ((), ()))
-    l01 = lax.dot_general(xpb[0], dgu[...], over_rows, preferred_element_type=F32)
-    lsend[0] = l01[:, 0:HF].astype(BF)
-    lsend[1] = l01[:, HF : 2 * HF].astype(BF)
-    lsend[2] = lax.dot_general(xpb[1], hid[...], over_rows, preferred_element_type=F32).astype(BF)
-
     plane = [(dx, dy) for dy in range(NY) for dx in range(NX) if (dx, dy) != (0, 0)]
     far_first = sorted(plane, key=lambda t: -(min(t[0], NX - t[0]) + min(t[1], NY - t[1])))
 
@@ -320,17 +322,34 @@
     def rows_of(q):
         return pl.ds(al(q * NZ, NZ), NZ)
 
-    for dx, dy in far_first:
-        q = part_of(dx, dy)
-        both.start(lsend.at[:, rows_of(q)], lrecv.at[p, c], rsem.at[c, back(dx, dy)], dev(dx=dx, dy=dy, lead=True), part)
+    over_rows = (((0,), (0,)), ((), ()))
+    parted = []
+    for turn, hh in enumerate((c, o)):
+        ranks = hc if turn == 0 else ho
+        if turn == 1:
+            arrived(xpb.at[:, :, ho], psem.at[5])
+        l01 = lax.dot_general(xpb[0, :, ranks], dgu[...], over_rows, preferred_element_type=F32)
+        lsend[0, ranks, :] = l01[:, 0:HF].astype(BF)
+        lsend[1, ranks, :] = l01[:, HF : 2 * HF].astype(BF)
+        lsend[2, ranks, :] = lax.dot_general(
+            xpb[1, :, ranks], hid[...], over_rows, preferred_element_type=F32
+        ).astype(BF)
+        for i in range(8):
+            q = hh * 8 + lax.rem(p + i, 8)
+            away = jnp.logical_or(helps, q != p)
+            parted.append(away)
+
+            @pl.when(away)
+            def _():
+                pltpu.make_async_remote_copy(
+                    src_ref=lsend.at[:, rows_of(q)], dst_ref=lrecv.at[p, c],
+                    send_sem=part_sem.at[8 * turn + i], recv_sem=rsem.at[c, p],
+                    device_id=(q, leaders[0]), device_id_type=MESH,
+                ).start()
 
     @pl.when(leads)
     def _():
         lrecv[p, 1] = lsend[:, rows_of(p)]
-
-    @pl.when(helps)
-    def _():
-        helper.start(lsend.at[:, rows_of(p)], lrecv.at[p, 0], rsem.at[0, 0], partner, part)
 
     def dx_part(core, put):
         lhs = dgu[pl.ds(al(core * TOK, TOK), TOK), :]
@@ -354,8 +373,8 @@
     def _():
         for half in (0, 1):
             for dx, dy in plane:
-                arrived(lrecv.at[part_of(dx, dy), half], rsem.at[half, dy * NX + dx])
-        arrived(lrecv.at[p, 0], rsem.at[0, 0])
+                arrived(lrecv.at[part_of(dx, dy), half], rsem.at[half, part_of(dx, dy)])
+        arrived(lrecv.at[p, 0], rsem.at[0, p])
         total = lrecv[0].astype(F32)
         for q in range(1, NP):
             total = total + lrecv[q].astype(F32)
@@ -463,6 +482,14 @@
 
     both.drain()
     gather.drain()
+    for i, away in enumerate(parted):
+
+        @pl.when(away)
+        def _():
+            pltpu.make_async_remote_copy(
+                src_ref=part(), dst_ref=part(), send_sem=part_sem.at[i], recv_sem=rsem.at[0, 0],
+                device_id=partner, device_id_type=MESH,
+            ).wait_send()
 
 
 def local(tokens, cotangent, w_gate, w_up, w_down, basis, first_moment, second_moment):
@@ -484,7 +511,7 @@
         v((NP, 1, HF), F32), v((8, HF), F32),
         v((8, FF), F32), v((NP, 8, FF), F32), v((8, 8, FF), F32),
         v((3, RANK, FF), BF), v((3, ROWS, FF), F32),
-        dma((8,)), dma((NLEAD,)), dma((NBOTH,)), dma((NHELP,)), dma((NGATHER,)), dma((2, NZ)), dma((2, 3, NZ)), dma((11,)),
+        dma((8,)), dma((NLEAD,)), dma((NBOTH,)), dma((NHELP,)), dma((NGATHER,)), dma((NP,)), dma((2, NZ)), dma((2, 3, NZ)), dma((11,)),
         dma((NZ,)), dma((2, NP)), dma((3,)), dma((3,)), dma((NP,)), dma((NP,)), dma((NP,)),
     ]
     kept = [((TOK, D), BF), ((3, 8, FF), F32), ((3, 8, FF), F32), ((3, ROWS, FF), F32)]

time: 79.6 us -> 78 us (0.980)
  Pallas kernels: 78.8 us -> 77.2 us
    pallas_call x1, Pallas kernels: 77.8 us -> 76.2 us  [local(): pl.pallas_call(kernel, out_shape=tuple((pltpu.VMEM(*k) for k in kept)), i...]
where the time goes in v4:
time: 78 us; the launch traced here: 77.8 us
  Pallas kernels  77.2 us (99%)
    pallas_call x1, Pallas kernels, local(): pl.pallas_call(kernel, out_shape=tuple((pltpu.VMEM(*k) for k in kept)), i...  76.2 us

profile of v4, /device:TPU:1, one launch (start us, length us, event | category | flops | bytes accessed | tf_op | source)
XLA Modules:
  0.0 77.8 jit_solution(3453744651857761923)
XLA Ops:
  0.6 76.2 %shard_map.111 = (bf16[128,2048]{1,0:T(8,128)(2,1)S(1)}, f32[3,8,512]{2,1,0:T(8,128)S(1)}, f32[3,8,512]{2,1,0:T(8,128)S(1)}, f32[3,64,512]{2,1,0:T(8,128)S(1)}) custom-call(bf16[128,2048]{1,0:T(8,128)(2,1)} %tok_hbm.1, bf16[128,2048]{1,0:T(8,128)(2,1)} %cot_hbm.1, bf16[64,512]{1,0:T(8,128)(2,1)} %wg_hbm.1, bf16[64,512]{1,0:T(8,128)(2,1)} %wu_hbm.1, ...), custom_call_target="tpu_custom_call" | custom-call | tf_op jit(solution)/shard_map/pallas_call | solution.py:519
  76.8 1.0 %shard_map.112 = (bf16[128,2048]{1,0:T(8,128)(2,1)}, f32[3,8,512]{2,1,0:T(8,128)}, f32[3,8,512]{2,1,0:T(8,128)}, f32[3,64,512]{2,1,0:T(8,128)}) custom-call(bf16[128,2048]{1,0:T(8,128)(2,1)S(1)} %get-tuple-element.8.a, f32[3,8,512]{2,1,0:T(8,128)S(1)} %get-tuple-element.9.b, f32[3,8,512]{2,1,0:T(8,128)S(1)} %get-tuple-element.10.c, ...), custom_call_target="tpu_custom_call" | custom-call | tf_op jit(solution)/shard_map/pallas_call | solution.py:529

commit v5 on v4

--- a/solution.py
+++ b/solution.py
@@ -204,14 +204,14 @@
 
     def z_arrive(s):
         later = PLAN.get(s, ())
-        for h in (0, 1):
+        for h, row in ((c, own_off), (o, oth_off)) if s < 6 else ((0, roff(0)), (1, roff(1))):
             for d in (0, 1) if s < 8 else (h,):
                 rel = s if d == 0 else NZ - s
                 sgn = 1 if d == 0 else -1
-                arrived(held(origin(rel), roff(h)), zsem.at[h, rel])
+                arrived(held(origin(rel), row), zsem.at[h, rel])
                 for t in later[:1]:
-                    if t < 8 or h == d:
-                        zsend(origin(rel), h, roff(h), sgn * (t - s), (rel + sgn * (t - s)) % NZ)
+                    if s < 6 or t < 8 or h == d:
+                        zsend(origin(rel), h, row, sgn * (t - s), (rel + sgn * (t - s)) % NZ)
         for h in (0, 1):
             for d in (0, 1):
                 rel = s if d == 0 else NZ - s

time: 78 us -> 77.7 us (level)
  no operation moved by 1% of the time
where the time goes in v5:
time: 77.7 us; the launch traced here: 77.5 us
  Pallas kernels  76.9 us (99%)
    pallas_call x1, Pallas kernels, local(): pl.pallas_call(kernel, out_shape=tuple((pltpu.VMEM(*k) for k in kept)), i...  75.9 us

profile of v5, /device:TPU:1, one launch (start us, length us, event | category | flops | bytes accessed | tf_op | source)
XLA Modules:
  0.0 77.5 jit_solution(9575913297458275685)
XLA Ops:
  0.6 75.9 %shard_map.111 = (bf16[128,2048]{1,0:T(8,128)(2,1)S(1)}, f32[3,8,512]{2,1,0:T(8,128)S(1)}, f32[3,8,512]{2,1,0:T(8,128)S(1)}, f32[3,64,512]{2,1,0:T(8,128)S(1)}) custom-call(bf16[128,2048]{1,0:T(8,128)(2,1)} %tok_hbm.1, bf16[128,2048]{1,0:T(8,128)(2,1)} %cot_hbm.1, bf16[64,512]{1,0:T(8,128)(2,1)} %wg_hbm.1, bf16[64,512]{1,0:T(8,128)(2,1)} %wu_hbm.1, ...), custom_call_target="tpu_custom_call" | custom-call | tf_op jit(solution)/shard_map/pallas_call | solution.py:519
  76.6 1.0 %shard_map.112 = (bf16[128,2048]{1,0:T(8,128)(2,1)}, f32[3,8,512]{2,1,0:T(8,128)}, f32[3,8,512]{2,1,0:T(8,128)}, f32[3,64,512]{2,1,0:T(8,128)}) custom-call(bf16[128,2048]{1,0:T(8,128)(2,1)S(1)} %get-tuple-element.8.a, f32[3,8,512]{2,1,0:T(8,128)S(1)} %get-tuple-element.9.b, f32[3,8,512]{2,1,0:T(8,128)S(1)} %get-tuple-element.10.c, ...), custom_call_target="tpu_custom_call" | custom-call | tf_op jit(solution)/shard_map/pallas_call | solution.py:529
